TPU v7x, 128 devices: a whole 4x4x4 slice. The times are simulated.
128 devices in a mesh: row: 16 (over y_hi, x, core), col: 8 (over z, y_lo).
Axes of the slice: x: 4, y: 4 (y_hi: 2, y_lo: 2; y = y_hi * 2 + y_lo), z: 4, core: 2. Of those that a mesh axis runs over, the one named last changes fastest.
Arguments:
- residual: bfloat16 [16, 8, 2048, 512], P('row', 'col'), may hold values from -6 to 6
- self_tiles: bfloat16 [16, 8, 2048, 2048], P('row', 'col'), may hold values from -0.09375 to 0.09375
- side_tiles: bfloat16 [16, 8, 2048, 2048], P('row', 'col'), may hold values from -0.09375 to 0.09375
- row_cluster_basis: bfloat16 [16, 8, 2048, 32], P('row', 'col'), may hold values from -0.125 to 0.125
- column_cluster_basis: bfloat16 [16, 8, 2048, 32], P('row', 'col'), may hold values from -1 to 1
- couplings: bfloat16 [16, 8, 64, 32, 32], P('row', 'col'), may hold values from -0.1875 to 0.1875
- near_side: int32 [16, 8], P('row', 'col'), may hold values from -1 to 1
- adm_targets: int32 [16, 8, 64], P('row', 'col'), may hold values from 0 to 127, as said below
- adm_ranks: int32 [16, 8, 64], P('row', 'col'), may hold values from 8 to 32
- adm_count: int32 [16, 8], P('row', 'col'), may hold values from 1 to 64
Outputs:
- gradient: float32 [16, 8, 2048, 512], P('row', 'col')
Inputs may be any that keep to these rules, and one draw needn't show every extreme that they name: `near_side`: -1 or +1 names the cluster row before or after around the loop of 16 rows; 0 means no such tile. Each entry of adm_targets for the block row of linear index i is the linear index of a cluster other than i; slot 0 names i - 1 or i + 1, counted round the 128 clusters; targets may repeat.
All inputs are finite; a program needn't handle non-finite values.
Results may differ from a plain program's by a relative error of at most 0.0033.
Values may be sent and summed in bfloat16 or wider, within the bound.
A program may use at most 128 MiB of HBM per device.

v0:
```python
import jax
import jax.numpy as jnp
from jax import lax
from jax.sharding import Mesh
from jax.sharding import PartitionSpec as P

ROW = ("row_0", "row_1", "row_2")
COL = ("col_0", "col_1")
ROW_COL = ("row_0", "row_1", "row_2", "col_0", "col_1")


def with_halo(block, sides, width):
    for axis, dim in sides:
        count = lax.axis_size(axis)
        forward = [(i, i + 1) for i in range(count - 1)]
        forward.append((count - 1, 0))
        backward = [(target, source) for source, target in forward]
        low = lax.ppermute(
            lax.slice_in_dim(block, block.shape[dim] - width, None, axis=dim), axis, forward
        )
        high = lax.ppermute(lax.slice_in_dim(block, 0, width, axis=dim), axis, backward)
        block = jnp.concatenate([low, block, high], axis=dim)
    return block


def cut_rows(length, count):
    unit = 8 if length >= 8 * count else 1
    return [length // unit * k // count * unit for k in range(1, count)]


def all_blocks(value, axes, sequence):
    pieces = value[None]
    for k in sequence:
        pieces = lax.all_gather(pieces, axes[k], axis=0, tiled=True)
    held = [lax.axis_size(axes[k]) for k in reversed(sequence)]
    pieces = pieces.reshape(*held, *value.shape)
    turned = sorted(range(len(sequence)), key=lambda place: sequence[len(sequence) - 1 - place])
    return pieces.transpose(*turned, *range(len(sequence), pieces.ndim)).reshape(-1, *value.shape)


def in_order(pieces, dim):
    pieces = jnp.moveaxis(pieces, 0, dim)
    dims = pieces.shape
    return pieces.reshape(*dims[:dim], dims[dim] * dims[dim + 1], *dims[dim + 2 :])


def gather_at_once(value, axes, dim):
    split_at = max(range(max(1, value.ndim - 1)), key=lambda d: value.shape[d])
    count, done = (len(axes), [])
    for initial, slab in enumerate(
        jnp.split(value, cut_rows(value.shape[split_at], count), axis=split_at)
    ):
        if slab.size:
            sequence = [(initial - k) % count for k in range(count)]
            done.append(all_blocks(slab, axes, sequence))
    return in_order(jnp.concatenate(done, axis=split_at + 1), dim)


def contract(tile, values):
    return lax.dot_general(
        tile, values, (((0,), (0,)), ((), ())), preferred_element_type=jnp.float32
    )


def on_device(
    residual,
    self_tiles,
    side_tiles,
    row_cluster_basis,
    column_cluster_basis,
    couplings,
    near_side,
    adm_targets,
    adm_ranks,
    adm_count,
):
    slot_count = couplings.shape[2]
    rank_dimension = couplings.shape[3]
    cluster_groups = lax.axis_size(ROW) * lax.axis_size(COL)
    local_rows = residual[0, 0]
    coefficient_table = contract(row_cluster_basis[0, 0], local_rows).astype(jnp.bfloat16)
    rank_index = jnp.arange(rank_dimension, dtype=jnp.int32)
    slot_index = jnp.arange(slot_count, dtype=jnp.int32)
    keep_mask = (rank_index[None, :] < adm_ranks[0, 0][:, None]) & (slot_index < adm_count[0, 0])[
        :, None
    ]
    keep_float = keep_mask.astype(jnp.float32)
    masked = couplings[0, 0].astype(jnp.float32) * keep_float[:, :, None] * keep_float[:, None, :]
    onehot = (
        adm_targets[0, 0][:, None] == jnp.arange(cluster_groups, dtype=jnp.int32)[None, :]
    ).astype(jnp.float32)
    coupled_blocks = lax.dot_general(
        onehot,
        masked.reshape(slot_count, rank_dimension * rank_dimension),
        (((0,), (0,)), ((), ())),
        precision=lax.Precision.HIGHEST,
        preferred_element_type=jnp.float32,
    )
    coupled_blocks = coupled_blocks.reshape(cluster_groups, rank_dimension, rank_dimension)
    padded = with_halo(residual, ((ROW, 0),), 1)
    side_offset = near_side[0, 0]
    neighbour = lax.dynamic_index_in_dim(padded, side_offset + 1, 0, keepdims=False)[0]
    own_part = contract(self_tiles[0, 0], local_rows)
    side_part = contract(side_tiles[0, 0], neighbour) * (side_offset != 0).astype(jnp.float32)
    received = lax.all_to_all(
        coupled_blocks.astype(jnp.bfloat16), ROW_COL, split_axis=0, concat_axis=0, tiled=True
    ).astype(coupled_blocks.dtype)
    dual_sums = jnp.einsum(
        "cab,can->bn",
        received,
        gather_at_once(coefficient_table[None], ROW_COL, 0).astype(jnp.float32),
        precision=lax.Precision.HIGHEST,
    )
    dual_vector = dual_sums.astype(jnp.bfloat16)
    distant_part = jnp.dot(
        column_cluster_basis[0, 0], dual_vector, preferred_element_type=jnp.float32
    )
    gradient = own_part + side_part + distant_part
    return gradient[None, None]


def solution(mesh):
    torus = Mesh(mesh.devices.reshape(2, 4, 2, 4, 2), ("row_0", "row_1", "row_2", "col_0", "col_1"))
    in_specs = (
        P(ROW, COL, None, None),
        P(ROW, COL, None, None),
        P(ROW, COL, None, None),
        P(ROW, COL, None, None),
        P(ROW, COL, None, None),
        P(ROW, COL, None, None, None),
        P(ROW, COL),
        P(ROW, COL, None),
        P(ROW, COL, None),
        P(ROW, COL),
    )
    out_specs = P(ROW, COL, None, None)
    return jax.shard_map(
        on_device, mesh=torus, in_specs=in_specs, out_specs=out_specs, check_vma=False
    )
```

profile of v0, /device:TPU:40, one launch (start us, length us, event | category | flops | bytes accessed | tf_op | source)
XLA Modules:
  0.0 274.3 jit_solution(9813288460616339119)
XLA Ops:
  0.0 0.0 copy-start
  0.0 0.0 collective-permute-start
  0.0 5.3 %collective-permute-start.1 = (bf16[1,1,2048,512]{3,2,1,0:T(8,128)(2,1)}, bf16[1,1,2048,512]{3,2,1,0:T(8,128)(2,1)}, u32[]{:S(2)}, u32[]{:S(2)}) collective-permute-start(bf16[1,1,2048,512]{3,2,1,0:T(8,128)(2,1)} %param.10), channel_id=1, source_target_pairs={{8,0},{16,8},{24,16},{32,24},{40,32},{48,40},{56,48},{64,56},{72,6... | collective-permute-start | bytes 6291464 | tf_op jit(solution)/shard_map/ppermute | solution.py:21
  6.0 0.7 fusion.37
  6.7 1.0 fusion.29
  7.7 1.1 convolution_convert_fusion
  8.8 1.4 copy.40
  10.2 1.5 reshape.163
  11.8 8.2 %all-to-all-start = ((bf16[128,2,512]{2,1,0:T(2,128)(2,1)}), bf16[128,2,512]{2,1,0:T(2,128)(2,1)}, u32[]{:S(2)}, u32[]{:S(2)}) async-start(bf16[128,2,512]{2,1,0:T(2,128)(2,1)} %reshape.163), calls=%async_computation | async-start | bytes 524288 | tf_op jit(solution)/shard_map/all_to_all | solution.py:105
  20.0 0.0 copy-done.1
  20.0 1.4 fusion.25
  21.4 11.0 %all-gather = bf16[2,6,512]{2,1,0:T(8,128)(2,1)S(1)} all-gather(bf16[1,6,512]{2,1,0:T(8,128)(2,1)S(1)} %get-tuple-element.9), channel_id=2, replica_groups=mesh['row_0'=2,'row_1'=4,'row_2'=2,'col_0'=4,'col_1'=2] {'row_0'}, dimensions={0}, use_global_device_ids=true | all-gather | bytes 18432 | tf_op jit(solution)/shard_map/all_gather | solution.py:34
  32.4 4.4 %all-gather.1 = bf16[4,6,512]{2,1,0:T(8,128)(2,1)S(1)} all-gather(bf16[2,6,512]{2,1,0:T(8,128)(2,1)S(1)} %all-gather), channel_id=3, replica_groups=mesh['row_0'=2,'row_1'=4,'row_2'=2,'col_0'=4,'col_1'=2] {'col_1'}, dimensions={0}, use_global_device_ids=true | all-gather | bytes 36864 | tf_op jit(solution)/shard_map/all_gather | solution.py:34
  36.8 12.9 %all-gather.2 = bf16[16,6,512]{2,1,0:T(8,128)(2,1)S(1)} all-gather(bf16[4,6,512]{2,1,0:T(8,128)(2,1)S(1)} %all-gather.1), channel_id=4, replica_groups=mesh['row_0'=2,'row_1'=4,'row_2'=2,'col_0'=4,'col_1'=2] {'col_0'}, dimensions={0}, use_global_device_ids=true | all-gather | bytes 122880 | tf_op jit(solution)/shard_map/all_gather | solution.py:34
  49.7 1.9 all-gather.3
  51.7 16.2 %all-gather.4 = bf16[128,6,512]{2,0,1:T(8,128)(2,1)S(1)} all-gather(bf16[32,6,512]{2,0,1:T(8,128)(2,1)S(1)} %all-gather.3), channel_id=6, replica_groups=mesh['row_0'=2,'row_1'=4,'row_2'=2,'col_0'=4,'col_1'=2] {'row_1'}, dimensions={0}, use_global_device_ids=true | all-gather | bytes 983040 | tf_op jit(solution)/shard_map/all_gather | solution.py:34
  67.8 0.3 reshape.121
  68.1 0.9 copy.63
  69.0 0.3 reshape.122
  69.3 0.9 constant_dynamic-update-slice_fusion.3
  70.2 12.2 %all-gather.5 = bf16[4,6,512]{2,1,0:T(8,128)(2,1)S(1)} all-gather(bf16[1,6,512]{2,1,0:T(8,128)(2,1)S(1)} %get-tuple-element.8), channel_id=7, replica_groups=mesh['row_0'=2,'row_1'=4,'row_2'=2,'col_0'=4,'col_1'=2] {'row_1'}, dimensions={0}, use_global_device_ids=true | all-gather | bytes 30720 | tf_op jit(solution)/shard_map/all_gather | solution.py:34
  82.4 6.1 %all-gather.6 = bf16[8,6,512]{2,1,0:T(8,128)(2,1)S(1)} all-gather(bf16[4,6,512]{2,1,0:T(8,128)(2,1)S(1)} %all-gather.5), channel_id=8, replica_groups=mesh['row_0'=2,'row_1'=4,'row_2'=2,'col_0'=4,'col_1'=2] {'row_0'}, dimensions={0}, use_global_device_ids=true | all-gather | bytes 73728 | tf_op jit(solution)/shard_map/all_gather | solution.py:34
  88.5 4.8 %all-gather.7 = bf16[16,6,512]{2,0,1:T(8,128)(2,1)S(1)} all-gather(bf16[8,6,512]{2,0,1:T(8,128)(2,1)S(1)} %copy.43), channel_id=9, replica_groups=mesh['row_0'=2,'row_1'=4,'row_2'=2,'col_0'=4,'col_1'=2] {'col_1'}, dimensions={0}, use_global_device_ids=true | all-gather | bytes 147456 | tf_op jit(solution)/shard_map/all_gather | solution.py:34
  93.3 12.5 %all-gather.8 = bf16[64,6,512]{2,0,1:T(8,128)(2,1)S(1)} all-gather(bf16[16,6,512]{2,0,1:T(8,128)(2,1)S(1)} %all-gather.7), channel_id=10, replica_groups=mesh['row_0'=2,'row_1'=4,'row_2'=2,'col_0'=4,'col_1'=2] {'col_0'}, dimensions={0}, use_global_device_ids=true | all-gather | bytes 491520 | tf_op jit(solution)/shard_map/all_gather | solution.py:34
  105.8 2.4 all-gather.9
  108.2 0.2 reshape.123
  108.4 0.8 copy.62
  109.2 0.3 reshape.124
  109.5 1.8 all-gather.10
  111.3 11.9 %all-gather.11 = bf16[8,7,512]{2,1,0:T(8,128)(2,1)S(1)} all-gather(bf16[2,7,512]{2,1,0:T(8,128)(2,1)S(1)} %all-gather.10), channel_id=13, replica_groups=mesh['row_0'=2,'row_1'=4,'row_2'=2,'col_0'=4,'col_1'=2] {'row_1'}, dimensions={0}, use_global_device_ids=true | all-gather | bytes 71680 | tf_op jit(solution)/shard_map/all_gather | solution.py:34
  123.2 7.0 %all-gather.12 = bf16[16,7,512]{2,0,1:T(8,128)(2,1)S(1)} all-gather(bf16[8,7,512]{2,0,1:T(8,128)(2,1)S(1)} %copy.45), channel_id=14, replica_groups=mesh['row_0'=2,'row_1'=4,'row_2'=2,'col_0'=4,'col_1'=2] {'row_0'}, dimensions={0}, use_global_device_ids=true | all-gather | bytes 172032 | tf_op jit(solution)/shard_map/all_gather | solution.py:34
  130.1 5.4 %all-gather.13 = bf16[32,7,512]{2,0,1:T(8,128)(2,1)S(1)} all-gather(bf16[16,7,512]{2,0,1:T(8,128)(2,1)S(1)} %all-gather.12), channel_id=15, replica_groups=mesh['row_0'=2,'row_1'=4,'row_2'=2,'col_0'=4,'col_1'=2] {'col_1'}, dimensions={0}, use_global_device_ids=true | all-gather | bytes 344064 | tf_op jit(solution)/shard_map/all_gather | solution.py:34
  135.6 13.9 %all-gather.14 = bf16[128,7,512]{2,0,1:T(8,128)(2,1)S(1)} all-gather(bf16[32,7,512]{2,0,1:T(8,128)(2,1)S(1)} %all-gather.13), channel_id=16, replica_groups=mesh['row_0'=2,'row_1'=4,'row_2'=2,'col_0'=4,'col_1'=2] {'col_0'}, dimensions={0}, use_global_device_ids=true | all-gather | bytes 1146880 | tf_op jit(solution)/shard_map/all_gather | solution.py:34
  149.5 0.3 reshape.125
  149.8 0.9 copy.60
  150.8 0.3 reshape.126
  151.1 11.9 %all-gather.15 = bf16[4,6,512]{2,1,0:T(8,128)(2,1)S(1)} all-gather(bf16[1,6,512]{2,1,0:T(8,128)(2,1)S(1)} %get-tuple-element.7), channel_id=17, replica_groups=mesh['row_0'=2,'row_1'=4,'row_2'=2,'col_0'=4,'col_1'=2] {'col_0'}, dimensions={0}, use_global_device_ids=true | all-gather | bytes 30720 | tf_op jit(solution)/shard_map/all_gather | solution.py:34
  163.0 1.8 all-gather.16
  164.9 12.1 %all-gather.17 = bf16[32,6,512]{2,0,1:T(8,128)(2,1)S(1)} all-gather(bf16[8,6,512]{2,0,1:T(8,128)(2,1)S(1)} %copy.47), channel_id=19, replica_groups=mesh['row_0'=2,'row_1'=4,'row_2'=2,'col_0'=4,'col_1'=2] {'row_1'}, dimensions={0}, use_global_device_ids=true | all-gather | bytes 245760 | tf_op jit(solution)/shard_map/all_gather | solution.py:34
  177.0 8.4 %all-gather.18 = bf16[64,6,512]{2,0,1:T(8,128)(2,1)S(1)} all-gather(bf16[32,6,512]{2,0,1:T(8,128)(2,1)S(1)} %all-gather.17), channel_id=20, replica_groups=mesh['row_0'=2,'row_1'=4,'row_2'=2,'col_0'=4,'col_1'=2] {'row_0'}, dimensions={0}, use_global_device_ids=true | all-gather | bytes 589824 | tf_op jit(solution)/shard_map/all_gather | solution.py:34
  185.5 8.5 %all-gather.19 = bf16[128,6,512]{2,0,1:T(8,128)(2,1)S(1)} all-gather(bf16[64,6,512]{2,0,1:T(8,128)(2,1)S(1)} %all-gather.18), channel_id=21, replica_groups=mesh['row_0'=2,'row_1'=4,'row_2'=2,'col_0'=4,'col_1'=2] {'col_1'}, dimensions={0}, use_global_device_ids=true | all-gather | bytes 1179648 | tf_op jit(solution)/shard_map/all_gather | solution.py:34
  194.0 0.2 reshape.127
  194.2 1.1 copy.61
  195.3 0.3 reshape.128
  195.6 4.4 %all-gather.20 = bf16[2,7,512]{2,1,0:T(8,128)(2,1)S(1)} all-gather(bf16[1,7,512]{2,1,0:T(8,128)(2,1)S(1)} %get-tuple-element.5), channel_id=22, replica_groups=mesh['row_0'=2,'row_1'=4,'row_2'=2,'col_0'=4,'col_1'=2] {'col_1'}, dimensions={0}, use_global_device_ids=true | all-gather | bytes 21504 | tf_op jit(solution)/shard_map/all_gather | solution.py:34
  199.9 11.8 %all-gather.21 = bf16[8,7,512]{2,1,0:T(8,128)(2,1)S(1)} all-gather(bf16[2,7,512]{2,1,0:T(8,128)(2,1)S(1)} %all-gather.20), channel_id=23, replica_groups=mesh['row_0'=2,'row_1'=4,'row_2'=2,'col_0'=4,'col_1'=2] {'col_0'}, dimensions={0}, use_global_device_ids=true | all-gather | bytes 71680 | tf_op jit(solution)/shard_map/all_gather | solution.py:34
  211.8 1.9 all-gather.22
  213.7 13.2 %all-gather.23 = bf16[64,7,512]{2,0,1:T(8,128)(2,1)S(1)} all-gather(bf16[16,7,512]{2,0,1:T(8,128)(2,1)S(1)} %all-gather.22), channel_id=25, replica_groups=mesh['row_0'=2,'row_1'=4,'row_2'=2,'col_0'=4,'col_1'=2] {'row_1'}, dimensions={0}, use_global_device_ids=true | all-gather | bytes 573440 | tf_op jit(solution)/shard_map/all_gather | solution.py:34
  226.9 13.4 %all-gather.24 = bf16[128,7,512]{2,0,1:T(8,128)(2,1)S(1)} all-gather(bf16[64,7,512]{2,0,1:T(8,128)(2,1)S(1)} %all-gather.23), channel_id=26, replica_groups=mesh['row_0'=2,'row_1'=4,'row_2'=2,'col_0'=4,'col_1'=2] {'row_0'}, dimensions={0}, use_global_device_ids=true | all-gather | bytes 1376256 | tf_op jit(solution)/shard_map/all_gather | solution.py:34
  241.0 0.9 constant_dynamic-update-slice_fusion.2
  241.9 1.0 constant_dynamic-update-slice_fusion.1
  242.9 0.9 constant_dynamic-update-slice_fusion
  243.9 10.5 %fusion.2 = f32[2048,512]{1,0:T(8,128)} fusion(bf16[1,1,2048,2048]{3,2,1,0:T(8,128)(2,1)} %param.11, bf16[1,1,2048,512]{3,2,1,0:T(8,128)(2,1)} %param.10), kind=kOutput, calls=%fused_computation.2 | convolution fusion | flops 4294967296 | bytes 14680064 | tf_op jit(solution)/shard_map/dot_general | solution.py:60
  254.3 1.0 bitcast_dynamic-update-slice_fusion
  255.3 0.0 all-to-all-done
  255.3 1.9 reshape.164
  257.3 3.1 %fusion.19 = bf16[32,512]{1,0:T(8,128)(2,1)S(1)} fusion(bf16[128,1,32,512]{3,0,2,1:T(8,128)(2,1)} %bitcast_dynamic-update-slice_fusion, bf16[128,32,32]{2,1,0:T(8,128)(2,1)S(1)} %reshape.164), kind=kOutput, calls=%fused_computation.20 | convolution fusion | flops 134234112 | bytes 4489216 | tf_op jit(solution)/shard_map/cab,can->bn/dot_general | solution.py:108
  260.4 0.0 copy-done
  260.4 0.0 copy-start.2
  260.4 0.7 fusion.30
  261.2 0.0 collective-permute-done
  261.2 0.0 collective-permute-done.1
  261.2 0.8 copy-done.2
  262.0 12.3 %fusion.4 = f32[1,1,2048,512]{3,2,1,0:T(8,128)} fusion(f32[512,2048]{0,1:T(8,128)S(1)} %fusion.30, f32[2048,512]{1,0:T(8,128)} %fusion.2, bf16[1,1,2048,2048]{3,2,1,0:T(8,128)(2,1)} %param.12, s32[]{:T(128)S(6)} %select_n.4, bf16[1,1,2048,512]{3,2,1,0:T(8,128)(2,1)} %collective-permute-done, bf16[1,1,2048,512]{3,2,1,0:T(8,128)(2,1)S(1)} %copy-done.2, ...), kind=kOutput, calls=%fused_computation.8 | convolution fusion | flops 4300210176 | bytes 27262984 | tf_op jit(solution)/shard_map/dot_general | solution.py:60
  (9 shorter events, 0.2 us)
Async XLA Ops:
  0.0 260.4 %copy-start = (bf16[1,1,2048,32]{2,3,1,0:T(8,128)(2,1)S(1)}, bf16[1,1,2048,32]{2,3,1,0:T(8,128)(2,1)}, u32[]{:S(2)}) copy-start(bf16[1,1,2048,32]{2,3,1,0:T(8,128)(2,1)} %param.14) | copy-start | bytes 393220
  0.0 20.0 %copy-start.1 = (bf16[1,1,2048,512]{3,2,1,0:T(8,128)(2,1)S(1)}, bf16[1,1,2048,512]{3,2,1,0:T(8,128)(2,1)}, u32[]{:S(2)}) copy-start(bf16[1,1,2048,512]{3,2,1,0:T(8,128)(2,1)} %param.10) | copy-start | bytes 6291460
  0.0 261.2 %collective-permute-start = (bf16[1,1,2048,512]{3,2,1,0:T(8,128)(2,1)}, bf16[1,1,2048,512]{3,2,1,0:T(8,128)(2,1)}, u32[]{:S(2)}, u32[]{:S(2)}) collective-permute-start(bf16[1,1,2048,512]{3,2,1,0:T(8,128)(2,1)} %param.10), channel_id=1, source_target_pairs={{0,8},{8,16},{16,24},{24,32},{32,40},{40,48},{48,56},{56,64},{64,7... | collective-permute-start | bytes 6291464 | tf_op jit(solution)/shard_map/ppermute | solution.py:18
  0.0 261.2 %collective-permute-start.1 = (bf16[1,1,2048,512]{3,2,1,0:T(8,128)(2,1)}, bf16[1,1,2048,512]{3,2,1,0:T(8,128)(2,1)}, u32[]{:S(2)}, u32[]{:S(2)}) collective-permute-start(bf16[1,1,2048,512]{3,2,1,0:T(8,128)(2,1)} %param.10), channel_id=1, source_target_pairs={{8,0},{16,8},{24,16},{32,24},{40,32},{48,40},{56,48},{64,56},{72,6... | collective-permute-start | bytes 6291464 | tf_op jit(solution)/shard_map/ppermute | solution.py:21
  11.8 243.6 %all-to-all-start = ((bf16[128,2,512]{2,1,0:T(2,128)(2,1)}), bf16[128,2,512]{2,1,0:T(2,128)(2,1)}, u32[]{:S(2)}, u32[]{:S(2)}) async-start(bf16[128,2,512]{2,1,0:T(2,128)(2,1)} %reshape.163), calls=%async_computation | async-start | bytes 524288 | tf_op jit(solution)/shard_map/all_to_all | solution.py:105
  260.4 1.6 copy-start.2
where the time goes:
time: 275 us; the launch traced here: 274 us
  blocking collectives  212 us (77%)
  matrix products  29.1 us (11%)
  local copies, waits for them, and re-layouts  16.6 us (6%)
  starting transfers between devices  13.5 us (5%)
    all_gather x25, blocking collectives, all_blocks(): pieces = lax.all_gather(pieces, axes[k], axis=0, tiled=True)  212 us
    dot_general x3, matrix products, contract(): lax.dot_general(tile, values, (((0,), (0,)), ((), ())), preferred_element...  24.2 us
    all_to_all x1, starting transfers between devices, on_device(): lax.all_to_all(coupled_blocks.astype(jnp.bfloat16), ROW_COL, split_axis=0...  8.18 us
    unnamed x12, local copies, waits for them, and re-layouts  8.06 us
  transfers between devices with their start and end apart: 3, of which 0 were waited for; matrix products, arithmetic and copies ran while one was open for 12% of the time, Pallas kernels for 0%

commit v1 on v0

--- a/solution.py
+++ b/solution.py
@@ -31,7 +31,9 @@
 def all_blocks(value, axes, sequence):
     pieces = value[None]
     for k in sequence:
-        pieces = lax.all_gather(pieces, axes[k], axis=0, tiled=True)
+        pieces = jnp.concatenate(
+            lax.all_to_all(jnp.stack([pieces] * lax.axis_size(axes[k])), axes[k], 0, 0), axis=0
+        )
     held = [lax.axis_size(axes[k]) for k in reversed(sequence)]
     pieces = pieces.reshape(*held, *value.shape)
     turned = sorted(range(len(sequence)), key=lambda place: sequence[len(sequence) - 1 - place])

time: 275 us -> 332 us (1.21)
  blocking collectives: 212 us -> 28.6 us
  waiting for transfers between devices: 0.01 us -> 121 us
  starting transfers between devices: 13.5 us -> 93.7 us
  local copies, waits for them, and re-layouts: 16.6 us -> 47.6 us
  other arithmetic: 1.67 us -> 6.76 us
    all_gather x25 -> x0, blocking collectives: 212 us -> none  [all_blocks(): pieces = lax.all_gather(pieces, axes[k], axis=0, tiled=True)]
    all_to_all x0 -> x20, waiting for transfers between devices: none -> 111 us  [all_blocks(): lax.all_to_all(jnp.stack([pieces] * lax.axis_size(axes[k])), axes[k], 0, 0)]
    all_to_all x0 -> x20, starting transfers between devices: none -> 82 us  [all_blocks(): lax.all_to_all(jnp.stack([pieces] * lax.axis_size(axes[k])), axes[k], 0, 0)]
    all_to_all x0 -> x5, blocking collectives: none -> 28.6 us  [all_blocks(): lax.all_to_all(jnp.stack([pieces] * lax.axis_size(axes[k])), axes[k], 0, 0)]
    another operation x0 -> x23, local copies, waits for them, and re-layouts: none -> 11.2 us  [the longest x22 8.39 us: all_blocks(): jnp.stack([pieces] * lax.axis_size(axes[k]))]
    reshape x4, local copies, waits for them, and re-layouts: 1.25 us -> 11.3 us  [all_blocks(): pieces.transpose(*turned, *range(len(sequence), pieces.ndim))]
    all_to_all x1, waiting for transfers between devices: 0.01 us -> 9.67 us  [on_device(): lax.all_to_all(coupled_blocks.astype(jnp.bfloat16), ROW_COL, split_axis=0...]
    another operation x0 -> x15, other arithmetic: none -> 6.68 us  [all_blocks(): jnp.stack([pieces] * lax.axis_size(axes[k]))]
  transfers between devices with their start and end apart: 3 -> 23, of which waited for: 0 -> 19; matrix products, arithmetic and copies ran while one was open for 12% -> 19% of each run, Pallas kernels for 0% -> 0%
where the time goes in v1:
time: 332 us; the launch traced here: 328 us
  waiting for transfers between devices  121 us (36%)
  starting transfers between devices  93.7 us (28%)
  local copies, waits for them, and re-layouts  47.6 us (14%)
  matrix products  29.4 us (9%)
  blocking collectives  28.6 us (9%)
  other arithmetic  6.76 us (2%)
    all_to_all x20, waiting for transfers between devices, all_blocks(): lax.all_to_all(jnp.stack([pieces] * lax.axis_size(axes[k])), axes[k], 0, 0)  111 us
    all_to_all x20, starting transfers between devices, all_blocks(): lax.all_to_all(jnp.stack([pieces] * lax.axis_size(axes[k])), axes[k], 0, 0)  82 us
    all_to_all x5, blocking collectives, all_blocks(): lax.all_to_all(jnp.stack([pieces] * lax.axis_size(axes[k])), axes[k], 0, 0)  28.6 us
    dot_general x3, matrix products, contract(): lax.dot_general(tile, values, (((0,), (0,)), ((), ())), preferred_element...  25.1 us
    reshape x4, local copies, waits for them, and re-layouts, all_blocks(): pieces.transpose(*turned, *range(len(sequence), pieces.ndim))  11.3 us
    unnamed x22, local copies, waits for them, and re-layouts  11.1 us
    all_to_all x1, waiting for transfers between devices, on_device(): lax.all_to_all(coupled_blocks.astype(jnp.bfloat16), ROW_COL, split_axis=0...  9.67 us
    another operation x22, local copies, waits for them, and re-layouts, all_blocks(): jnp.stack([pieces] * lax.axis_size(axes[k]))  8.39 us
  transfers between devices with their start and end apart: 23, of which 19 were waited for; matrix products, arithmetic and copies ran while one was open for 19% of the time, Pallas kernels for 0%

profile of v1, /device:TPU:40, one launch (start us, length us, event | category | flops | bytes accessed | tf_op | source)
XLA Modules:
  0.0 328.3 jit_solution(16167904188411604946)
XLA Ops:
  0.0 2.2 fusion.25
  2.8 3.2 all-to-all-start.11
  7.4 3.6 %all-to-all-start.1 = ((bf16[2,1,1,6,512]{4,3,2,1,0:T(8,128)(2,1)}), bf16[2,1,1,6,512]{4,3,2,1,0:T(8,128)(2,1)S(1)}, u32[]{:S(2)}, u32[]{:S(2)}) async-start(bf16[2,1,1,6,512]{4,3,2,1,0:T(8,128)(2,1)} %pad_maximum_fusion.12), calls=%async_computation.1 | async-start | bytes 32768 | tf_op jit(solution)/shard_map/all_to_all | solution.py:35
  11.6 4.8 %all-to-all-done.1 = bf16[2,1,1,6,512]{4,3,2,1,0:T(8,128)(2,1)S(1)} async-done(((bf16[2,1,1,6,512]{4,3,2,1,0:T(8,128)(2,1)}), bf16[2,1,1,6,512]{4,3,2,1,0:T(8,128)(2,1)S(1)}, u32[]{:S(2)}, u32[]{:S(2)}) %all-to-all-start.1) | async-done | bytes 12320 | tf_op jit(solution)/shard_map/all_to_all | solution.py:35
  16.4 4.6 %all-to-all-start.21 = ((bf16[2,1,1,7,512]{4,3,2,1,0:T(8,128)(2,1)}), bf16[2,1,1,7,512]{4,3,2,1,0:T(8,128)(2,1)S(1)}, u32[]{:S(2)}, u32[]{:S(2)}) async-start(bf16[2,1,1,7,512]{4,3,2,1,0:T(8,128)(2,1)} %pad_maximum_fusion.14), calls=%async_computation.21 | async-start | bytes 32768 | tf_op jit(solution)/shard_map/all_to_all | solution.py:35
  21.0 1.8 all-to-all-done.21
  22.8 6.2 %all_to_all.130 = bf16[2,2,1,6,512]{4,1,3,2,0:T(2,128)(2,1)S(1)} all-to-all(bf16[2,2,1,6,512]{4,1,3,2,0:T(2,128)(2,1)S(1)} %copy.86), channel_id=1, replica_groups=mesh['row_0'=2,'row_1'=4,'row_2'=2,'col_0'=4,'col_1'=2] {'col_1'}, dimensions={0} | all-to-all | bytes 49152 | tf_op jit(solution)/shard_map/all_to_all | solution.py:35
  29.0 9.5 %all_to_all.131 = bf16[4,1,1,6,512]{4,3,2,1,0:T(8,128)(2,1)S(1)} all-to-all(bf16[4,1,1,6,512]{4,3,2,1,0:T(8,128)(2,1)S(1)} %stack.80), channel_id=1, replica_groups=mesh['row_0'=2,'row_1'=4,'row_2'=2,'col_0'=4,'col_1'=2] {'row_1'}, dimensions={0} | all-to-all | bytes 49152 | tf_op jit(solution)/shard_map/all_to_all | solution.py:35
  39.2 5.4 %all-to-all-start.16 = ((bf16[4,1,1,6,512]{4,3,2,1,0:T(8,128)(2,1)}), bf16[4,1,1,6,512]{4,3,2,1,0:T(8,128)(2,1)S(1)}, u32[]{:S(2)}, u32[]{:S(2)}) async-start(bf16[4,1,1,6,512]{4,3,2,1,0:T(8,128)(2,1)} %stack.90), calls=%async_computation.16 | async-start | bytes 65536 | tf_op jit(solution)/shard_map/all_to_all | solution.py:35
  45.2 3.3 %all-to-all-done.16 = bf16[4,1,1,6,512]{4,3,2,1,0:T(8,128)(2,1)S(1)} async-done(((bf16[4,1,1,6,512]{4,3,2,1,0:T(8,128)(2,1)}), bf16[4,1,1,6,512]{4,3,2,1,0:T(8,128)(2,1)S(1)}, u32[]{:S(2)}, u32[]{:S(2)}) %all-to-all-start.16) | async-done | bytes 24608 | tf_op jit(solution)/shard_map/all_to_all | solution.py:35
  48.6 3.3 all-to-all-start.7
  52.5 4.8 %all-to-all-done.7 = bf16[2,4,1,6,512]{4,1,3,2,0:T(4,128)(2,1)S(1)} async-done(((bf16[2,4,1,6,512]{4,1,3,2,0:T(4,128)(2,1)}), bf16[2,4,1,6,512]{4,1,3,2,0:T(4,128)(2,1)S(1)}, u32[]{:S(2)}, u32[]{:S(2)}) %all-to-all-start.7) | async-done | bytes 49184 | tf_op jit(solution)/shard_map/all_to_all | solution.py:35
  58.0 3.3 all-to-all-start.12
  62.1 4.8 %all-to-all-done.12 = bf16[4,2,1,7,512]{4,1,3,2,0:T(2,128)(2,1)S(1)} async-done(((bf16[4,2,1,7,512]{4,1,3,2,0:T(2,128)(2,1)}), bf16[4,2,1,7,512]{4,1,3,2,0:T(2,128)(2,1)S(1)}, u32[]{:S(2)}, u32[]{:S(2)}) %all-to-all-start.12) | async-done | bytes 57376 | tf_op jit(solution)/shard_map/all_to_all | solution.py:35
  67.5 4.7 %all-to-all-start.22 = ((bf16[4,2,1,7,512]{4,1,3,2,0:T(2,128)(2,1)}), bf16[4,2,1,7,512]{4,1,3,2,0:T(2,128)(2,1)S(1)}, u32[]{:S(2)}, u32[]{:S(2)}) async-start(bf16[4,2,1,7,512]{4,1,3,2,0:T(2,128)(2,1)} %stack.96), calls=%async_computation.22 | async-start | bytes 114688 | tf_op jit(solution)/shard_map/all_to_all | solution.py:35
  72.9 3.4 %all-to-all-done.22 = bf16[4,2,1,7,512]{4,1,3,2,0:T(2,128)(2,1)S(1)} async-done(((bf16[4,2,1,7,512]{4,1,3,2,0:T(2,128)(2,1)}), bf16[4,2,1,7,512]{4,1,3,2,0:T(2,128)(2,1)S(1)}, u32[]{:S(2)}, u32[]{:S(2)}) %all-to-all-start.22) | async-done | bytes 57376 | tf_op jit(solution)/shard_map/all_to_all | solution.py:35
  77.0 4.7 %all-to-all-start.3 = ((bf16[4,4,1,6,512]{4,1,3,2,0:T(4,128)(2,1)}), bf16[4,4,1,6,512]{4,1,3,2,0:T(4,128)(2,1)S(1)}, u32[]{:S(2)}, u32[]{:S(2)}) async-start(bf16[4,4,1,6,512]{4,1,3,2,0:T(4,128)(2,1)} %stack.77), calls=%async_computation.3 | async-start | bytes 196608 | tf_op jit(solution)/shard_map/all_to_all | solution.py:35
  81.8 4.2 %all-to-all-done.3 = bf16[4,4,1,6,512]{4,1,3,2,0:T(4,128)(2,1)S(1)} async-done(((bf16[4,4,1,6,512]{4,1,3,2,0:T(4,128)(2,1)}), bf16[4,4,1,6,512]{4,1,3,2,0:T(4,128)(2,1)S(1)}, u32[]{:S(2)}, u32[]{:S(2)}) %all-to-all-start.3) | async-done | bytes 98336 | tf_op jit(solution)/shard_map/all_to_all | solution.py:35
  86.1 3.3 all-to-all-start.17
  89.5 1.3 all-to-all-done.17
  90.8 3.8 %all_to_all.132 = bf16[2,8,1,7,512]{4,1,3,2,0:T(8,128)(2,1)S(1)} all-to-all(bf16[2,8,1,7,512]{4,1,3,2,0:T(8,128)(2,1)S(1)} %pad_maximum_fusion.7), channel_id=1, replica_groups=mesh['row_0'=2,'row_1'=4,'row_2'=2,'col_0'=4,'col_1'=2] {'row_2'}, dimensions={0} | all-to-all | bytes 229376 | tf_op jit(solution)/shard_map/all_to_all | solution.py:35
  94.6 3.9 %all_to_all.133 = bf16[2,16,1,6,512]{4,1,3,2,0:T(8,128)(2,1)S(1)} all-to-all(bf16[2,16,1,6,512]{4,1,3,2,0:T(8,128)(2,1)S(1)} %pad_maximum_fusion.5), channel_id=1, replica_groups=mesh['row_0'=2,'row_1'=4,'row_2'=2,'col_0'=4,'col_1'=2] {'row_2'}, dimensions={0} | all-to-all | bytes 393216 | tf_op jit(solution)/shard_map/all_to_all | solution.py:35
  98.5 5.3 %all-to-all-start.8 = ((bf16[2,8,1,6,512]{4,1,3,2,0:T(8,128)(2,1)}), bf16[2,8,1,6,512]{4,1,3,2,0:T(8,128)(2,1)S(1)}, u32[]{:S(2)}, u32[]{:S(2)}) async-start(bf16[2,8,1,6,512]{4,1,3,2,0:T(8,128)(2,1)} %pad_maximum_fusion.8), calls=%async_computation.8 | async-start | bytes 196608 | tf_op jit(solution)/shard_map/all_to_all | solution.py:35
  104.4 1.6 all-to-all-done.8
  106.1 3.4 %all-to-all-start.13 = ((bf16[2,8,1,7,512]{4,1,3,2,0:T(8,128)(2,1)}), bf16[2,8,1,7,512]{4,1,3,2,0:T(8,128)(2,1)S(1)}, u32[]{:S(2)}, u32[]{:S(2)}) async-start(bf16[2,8,1,7,512]{4,1,3,2,0:T(8,128)(2,1)} %pad_maximum_fusion.6), calls=%async_computation.13 | async-start | bytes 229376 | tf_op jit(solution)/shard_map/all_to_all | solution.py:35
  109.5 5.8 %all-to-all-done.13 = bf16[2,8,1,7,512]{4,1,3,2,0:T(8,128)(2,1)S(1)} async-done(((bf16[2,8,1,7,512]{4,1,3,2,0:T(8,128)(2,1)}), bf16[2,8,1,7,512]{4,1,3,2,0:T(8,128)(2,1)S(1)}, u32[]{:S(2)}, u32[]{:S(2)}) %all-to-all-start.13) | async-done | bytes 114720 | tf_op jit(solution)/shard_map/all_to_all | solution.py:35
  116.0 3.4 %all-to-all-start.18 = ((bf16[4,8,1,6,512]{4,1,3,2,0:T(8,128)(2,1)}), bf16[4,8,1,6,512]{4,1,3,2,0:T(8,128)(2,1)S(1)}, u32[]{:S(2)}, u32[]{:S(2)}) async-start(bf16[4,8,1,6,512]{4,1,3,2,0:T(8,128)(2,1)} %stack.92), calls=%async_computation.18 | async-start | bytes 393216 | tf_op jit(solution)/shard_map/all_to_all | solution.py:35
  120.2 5.5 %all-to-all-done.18 = bf16[4,8,1,6,512]{4,1,3,2,0:T(8,128)(2,1)S(1)} async-done(((bf16[4,8,1,6,512]{4,1,3,2,0:T(8,128)(2,1)}), bf16[4,8,1,6,512]{4,1,3,2,0:T(8,128)(2,1)S(1)}, u32[]{:S(2)}, u32[]{:S(2)}) %all-to-all-start.18) | async-done | bytes 196640 | tf_op jit(solution)/shard_map/all_to_all | solution.py:35
  125.7 5.4 %all-to-all-start.14 = ((bf16[2,16,1,7,512]{4,1,3,2,0:T(8,128)(2,1)}), bf16[2,16,1,7,512]{4,1,3,2,0:T(8,128)(2,1)S(1)}, u32[]{:S(2)}, u32[]{:S(2)}) async-start(bf16[2,16,1,7,512]{4,1,3,2,0:T(8,128)(2,1)} %pad_maximum_fusion.4), calls=%async_computation.14 | async-start | bytes 458752 | tf_op jit(solution)/shard_map/all_to_all | solution.py:35
  131.6 1.4 copy.85
  133.0 1.5 reshape.156
  134.5 6.2 %all-to-all-start = ((bf16[128,2,512]{2,1,0:T(2,128)(2,1)}), bf16[128,2,512]{2,1,0:T(2,128)(2,1)S(1)}, u32[]{:S(2)}, u32[]{:S(2)}) async-start(bf16[128,2,512]{2,1,0:T(2,128)(2,1)} %reshape.156), calls=%async_computation | async-start | bytes 524288 | tf_op jit(solution)/shard_map/all_to_all | solution.py:107
  140.8 9.7 %all-to-all-done = bf16[128,2,512]{2,1,0:T(2,128)(2,1)S(1)} async-done(((bf16[128,2,512]{2,1,0:T(2,128)(2,1)}), bf16[128,2,512]{2,1,0:T(2,128)(2,1)S(1)}, u32[]{:S(2)}, u32[]{:S(2)}) %all-to-all-start) | async-done | bytes 262176 | tf_op jit(solution)/shard_map/all_to_all | solution.py:107
  151.2 4.6 %all-to-all-start.9 = ((bf16[4,16,1,6,512]{4,1,3,2,0:T(8,128)(2,1)}), bf16[4,16,1,6,512]{4,1,3,2,0:T(8,128)(2,1)S(1)}, u32[]{:S(2)}, u32[]{:S(2)}) async-start(bf16[4,16,1,6,512]{4,1,3,2,0:T(8,128)(2,1)} %stack.83), calls=%async_computation.9 | async-start | bytes 786432 | tf_op jit(solution)/shard_map/all_to_all | solution.py:35
  156.6 5.3 %all-to-all-done.9 = bf16[4,16,1,6,512]{4,1,3,2,0:T(8,128)(2,1)S(1)} async-done(((bf16[4,16,1,6,512]{4,1,3,2,0:T(8,128)(2,1)}), bf16[4,16,1,6,512]{4,1,3,2,0:T(8,128)(2,1)S(1)}, u32[]{:S(2)}, u32[]{:S(2)}) %all-to-all-start.9) | async-done | bytes 393248 | tf_op jit(solution)/shard_map/all_to_all | solution.py:35
  161.9 3.5 %all-to-all-start.19 = ((bf16[2,32,1,6,512]{4,1,3,2,0:T(8,128)(2,1)}), bf16[2,32,1,6,512]{4,1,3,2,0:T(8,128)(2,1)S(1)}, u32[]{:S(2)}, u32[]{:S(2)}) async-start(bf16[2,32,1,6,512]{4,1,3,2,0:T(8,128)(2,1)} %pad_maximum_fusion.3), calls=%async_computation.19 | async-start | bytes 786432 | tf_op jit(solution)/shard_map/all_to_all | solution.py:35
  165.5 7.2 %all-to-all-done.19 = bf16[2,32,1,6,512]{4,1,3,2,0:T(8,128)(2,1)S(1)} async-done(((bf16[2,32,1,6,512]{4,1,3,2,0:T(8,128)(2,1)}), bf16[2,32,1,6,512]{4,1,3,2,0:T(8,128)(2,1)S(1)}, u32[]{:S(2)}, u32[]{:S(2)}) %all-to-all-start.19) | async-done | bytes 393248 | tf_op jit(solution)/shard_map/all_to_all | solution.py:35
  172.8 5.1 %all_to_all.134 = bf16[2,64,1,6,512]{4,1,3,2,0:T(8,128)(2,1)} all-to-all(bf16[2,64,1,6,512]{4,1,3,2,0:T(8,128)(2,1)S(1)} %pad_maximum_fusion.1), channel_id=1, replica_groups=mesh['row_0'=2,'row_1'=4,'row_2'=2,'col_0'=4,'col_1'=2] {'row_2'}, dimensions={0} | all-to-all | bytes 1572864 | tf_op jit(solution)/shard_map/all_to_all | solution.py:35
  178.7 3.5 %all-to-all-start.24 = ((bf16[4,16,1,7,512]{4,1,3,2,0:T(8,128)(2,1)}), bf16[4,16,1,7,512]{4,1,3,2,0:T(8,128)(2,1)S(1)}, u32[]{:S(2)}, u32[]{:S(2)}) async-start(bf16[4,16,1,7,512]{4,1,3,2,0:T(8,128)(2,1)} %stack.98), calls=%async_computation.24 | async-start | bytes 917504 | tf_op jit(solution)/shard_map/all_to_all | solution.py:35
  182.2 9.3 %all-to-all-done.24 = bf16[4,16,1,7,512]{4,1,3,2,0:T(8,128)(2,1)S(1)} async-done(((bf16[4,16,1,7,512]{4,1,3,2,0:T(8,128)(2,1)}), bf16[4,16,1,7,512]{4,1,3,2,0:T(8,128)(2,1)S(1)}, u32[]{:S(2)}, u32[]{:S(2)}) %all-to-all-start.24) | async-done | bytes 458784 | tf_op jit(solution)/shard_map/all_to_all | solution.py:35
  192.5 3.5 %all-to-all-start.5 = ((bf16[4,32,1,6,512]{4,1,3,2,0:T(8,128)(2,1)}), bf16[4,32,1,6,512]{4,1,3,2,0:T(8,128)(2,1)S(1)}, u32[]{:S(2)}, u32[]{:S(2)}) async-start(bf16[4,32,1,6,512]{4,1,3,2,0:T(8,128)(2,1)} %stack.79), calls=%async_computation.5 | async-start | bytes 1572864 | tf_op jit(solution)/shard_map/all_to_all | solution.py:35
  197.0 11.0 %all-to-all-done.5 = bf16[4,32,1,6,512]{4,1,3,2,0:T(8,128)(2,1)S(1)} async-done(((bf16[4,32,1,6,512]{4,1,3,2,0:T(8,128)(2,1)}), bf16[4,32,1,6,512]{4,1,3,2,0:T(8,128)(2,1)S(1)}, u32[]{:S(2)}, u32[]{:S(2)}) %all-to-all-start.5) | async-done | bytes 786464 | tf_op jit(solution)/shard_map/all_to_all | solution.py:35
  208.0 5.0 %all-to-all-start.20 = ((bf16[2,64,1,6,512]{4,1,3,2,0:T(8,128)(2,1)}), bf16[2,64,1,6,512]{4,1,3,2,0:T(8,128)(2,1)S(1)}, u32[]{:S(2)}, u32[]{:S(2)}) async-start(bf16[2,64,1,6,512]{4,1,3,2,0:T(8,128)(2,1)} %pad_maximum_fusion.2), calls=%async_computation.20 | async-start | bytes 1572864 | tf_op jit(solution)/shard_map/all_to_all | solution.py:35
  214.0 6.9 %all-to-all-done.20 = bf16[2,64,1,6,512]{4,1,3,2,0:T(8,128)(2,1)S(1)} async-done(((bf16[2,64,1,6,512]{4,1,3,2,0:T(8,128)(2,1)}), bf16[2,64,1,6,512]{4,1,3,2,0:T(8,128)(2,1)S(1)}, u32[]{:S(2)}, u32[]{:S(2)}) %all-to-all-start.20) | async-done | bytes 786464 | tf_op jit(solution)/shard_map/all_to_all | solution.py:35
  221.8 3.6 %all-to-all-start.25 = ((bf16[2,64,1,7,512]{4,1,3,2,0:T(8,128)(2,1)}), bf16[2,64,1,7,512]{4,1,3,2,0:T(8,128)(2,1)S(1)}, u32[]{:S(2)}, u32[]{:S(2)}) async-start(bf16[2,64,1,7,512]{4,1,3,2,0:T(8,128)(2,1)} %pad_maximum_fusion), calls=%async_computation.25 | async-start | bytes 1835008 | tf_op jit(solution)/shard_map/all_to_all | solution.py:35
  225.4 5.3 %collective-permute-start.1 = (bf16[1,1,2048,512]{3,2,1,0:T(8,128)(2,1)}, bf16[1,1,2048,512]{3,2,1,0:T(8,128)(2,1)}, u32[]{:S(2)}, u32[]{:S(2)}) collective-permute-start(bf16[1,1,2048,512]{3,2,1,0:T(8,128)(2,1)} %param.10), channel_id=1, source_target_pairs={{8,0},{16,8},{24,16},{32,24},{40,32},{48,40},{56,48},{64,56},{72,6... | collective-permute-start | bytes 6291464 | tf_op jit(solution)/shard_map/ppermute | solution.py:21
  230.8 29.0 %all-to-all-done.25 = bf16[2,64,1,7,512]{4,1,3,2,0:T(8,128)(2,1)S(1)} async-done(((bf16[2,64,1,7,512]{4,1,3,2,0:T(8,128)(2,1)}), bf16[2,64,1,7,512]{4,1,3,2,0:T(8,128)(2,1)S(1)}, u32[]{:S(2)}, u32[]{:S(2)}) %all-to-all-start.25) | async-done | bytes 917536 | tf_op jit(solution)/shard_map/all_to_all | solution.py:35
  260.8 4.9 %all-to-all-start.15 = ((bf16[4,32,1,7,512]{4,1,3,2,0:T(8,128)(2,1)}), bf16[4,32,1,7,512]{4,1,3,2,0:T(8,128)(2,1)S(1)}, u32[]{:S(2)}, u32[]{:S(2)}) async-start(bf16[4,32,1,7,512]{4,1,3,2,0:T(8,128)(2,1)} %stack.89), calls=%async_computation.15 | async-start | bytes 1835008 | tf_op jit(solution)/shard_map/all_to_all | solution.py:35
  265.8 10.6 %fusion.2 = f32[2048,512]{1,0:T(8,128)} fusion(bf16[1,1,2048,2048]{3,2,1,0:T(8,128)(2,1)} %param.11, bf16[1,1,2048,512]{3,2,1,0:T(8,128)(2,1)} %param.10), kind=kOutput, calls=%fused_computation.2 | convolution fusion | flops 4294967296 | bytes 14680064 | tf_op jit(solution)/shard_map/dot_general | solution.py:62
  277.5 1.9 copy.96
  279.4 1.7 copy.97
  281.1 3.0 reshape.148
  284.1 1.7 copy.90
  285.8 1.7 copy.91
  287.6 2.9 reshape.147
  290.5 2.1 constant_dynamic-update-slice_fusion.4
  292.6 2.1 constant_dynamic-update-slice_fusion.3
  294.7 2.8 copy.118
  297.6 3.0 reshape.150
  302.3 2.3 copy.103
  304.6 2.5 reshape.149
  308.1 2.1 constant_dynamic-update-slice_fusion.1
  311.2 3.1 fusion.19
  315.9 12.3 %fusion.4 = f32[1,1,2048,512]{3,2,1,0:T(8,128)} fusion(f32[512,2048]{0,1:T(8,128)S(1)} %fusion.30, f32[2048,512]{1,0:T(8,128)} %fusion.2, bf16[1,1,2048,2048]{3,2,1,0:T(8,128)(2,1)} %param.12, s32[]{:T(128)S(6)} %select_n.4, bf16[1,1,2048,512]{3,2,1,0:T(8,128)(2,1)} %collective-permute-done, bf16[1,1,2048,512]{3,2,1,0:T(8,128)(2,1)S(1)} %copy-done.4, ...), kind=kOutput, calls=%fused_computation.8 | convolution fusion | flops 4300210176 | bytes 27262984 | tf_op jit(solution)/shard_map/dot_general | solution.py:62
  (85 shorter events, 23.5 us)
Async XLA Ops:
  0.0 314.3 %copy-start = (bf16[1,1,2048,32]{2,3,1,0:T(8,128)(2,1)S(1)}, bf16[1,1,2048,32]{2,3,1,0:T(8,128)(2,1)}, u32[]{:S(2)}) copy-start(bf16[1,1,2048,32]{2,3,1,0:T(8,128)(2,1)} %param.14) | copy-start | bytes 393220
  0.0 119.4 %copy-start.6 = (s32[1,1,64]{2,1,0:T(1,128)S(1)}, s32[1,1,64]{2,1,0:T(1,128)}, u32[]{:S(2)}) copy-start(s32[1,1,64]{2,1,0:T(1,128)} %param.18) | copy-start | bytes 772
  0.0 119.4 %copy-start.5 = (bf16[1,1,64,32,32]{2,4,3,1,0:T(8,128)(2,1)S(1)}, bf16[1,1,64,32,32]{2,4,3,1,0:T(8,128)(2,1)}, u32[]{:S(2)}) copy-start(bf16[1,1,64,32,32]{2,4,3,1,0:T(8,128)(2,1)} %param.15) | copy-start | bytes 393220
  2.2 128.9 %copy-start.7 = (s32[1,1,64]{2,1,0:T(1,128)S(1)}, s32[1,1,64]{2,1,0:T(1,128)}, u32[]{:S(2)}) copy-start(s32[1,1,64]{2,1,0:T(1,128)} %param.17) | copy-start | bytes 772
  2.8 4.6 %all-to-all-start.11 = ((bf16[2,1,1,7,512]{4,3,2,1,0:T(8,128)(2,1)}), bf16[2,1,1,7,512]{4,3,2,1,0:T(8,128)(2,1)S(1)}, u32[]{:S(2)}, u32[]{:S(2)}) async-start(bf16[2,1,1,7,512]{4,3,2,1,0:T(8,128)(2,1)} %pad_maximum_fusion.13), calls=%async_computation.11 | async-start | bytes 32768 | tf_op jit(solution)/shard_map/all_to_all | solution.py:35
  7.4 8.9 %all-to-all-start.1 = ((bf16[2,1,1,6,512]{4,3,2,1,0:T(8,128)(2,1)}), bf16[2,1,1,6,512]{4,3,2,1,0:T(8,128)(2,1)S(1)}, u32[]{:S(2)}, u32[]{:S(2)}) async-start(bf16[2,1,1,6,512]{4,3,2,1,0:T(8,128)(2,1)} %pad_maximum_fusion.12), calls=%async_computation.1 | async-start | bytes 32768 | tf_op jit(solution)/shard_map/all_to_all | solution.py:35
  16.4 6.4 %all-to-all-start.21 = ((bf16[2,1,1,7,512]{4,3,2,1,0:T(8,128)(2,1)}), bf16[2,1,1,7,512]{4,3,2,1,0:T(8,128)(2,1)S(1)}, u32[]{:S(2)}, u32[]{:S(2)}) async-start(bf16[2,1,1,7,512]{4,3,2,1,0:T(8,128)(2,1)} %pad_maximum_fusion.14), calls=%async_computation.21 | async-start | bytes 32768 | tf_op jit(solution)/shard_map/all_to_all | solution.py:35
  39.2 9.4 %all-to-all-start.16 = ((bf16[4,1,1,6,512]{4,3,2,1,0:T(8,128)(2,1)}), bf16[4,1,1,6,512]{4,3,2,1,0:T(8,128)(2,1)S(1)}, u32[]{:S(2)}, u32[]{:S(2)}) async-start(bf16[4,1,1,6,512]{4,3,2,1,0:T(8,128)(2,1)} %stack.90), calls=%async_computation.16 | async-start | bytes 65536 | tf_op jit(solution)/shard_map/all_to_all | solution.py:35
  48.6 8.8 %all-to-all-start.7 = ((bf16[2,4,1,6,512]{4,1,3,2,0:T(4,128)(2,1)}), bf16[2,4,1,6,512]{4,1,3,2,0:T(4,128)(2,1)S(1)}, u32[]{:S(2)}, u32[]{:S(2)}) async-start(bf16[2,4,1,6,512]{4,1,3,2,0:T(4,128)(2,1)} %copy.92), calls=%async_computation.7 | async-start | bytes 98304 | tf_op jit(solution)/shard_map/all_to_all | solution.py:35
  58.0 8.8 %all-to-all-start.12 = ((bf16[4,2,1,7,512]{4,1,3,2,0:T(2,128)(2,1)}), bf16[4,2,1,7,512]{4,1,3,2,0:T(2,128)(2,1)S(1)}, u32[]{:S(2)}, u32[]{:S(2)}) async-start(bf16[4,2,1,7,512]{4,1,3,2,0:T(2,128)(2,1)} %stack.86), calls=%async_computation.12 | async-start | bytes 114688 | tf_op jit(solution)/shard_map/all_to_all | solution.py:35
  67.5 8.8 %all-to-all-start.22 = ((bf16[4,2,1,7,512]{4,1,3,2,0:T(2,128)(2,1)}), bf16[4,2,1,7,512]{4,1,3,2,0:T(2,128)(2,1)S(1)}, u32[]{:S(2)}, u32[]{:S(2)}) async-start(bf16[4,2,1,7,512]{4,1,3,2,0:T(2,128)(2,1)} %stack.96), calls=%async_computation.22 | async-start | bytes 114688 | tf_op jit(solution)/shard_map/all_to_all | solution.py:35
  77.0 9.1 %all-to-all-start.3 = ((bf16[4,4,1,6,512]{4,1,3,2,0:T(4,128)(2,1)}), bf16[4,4,1,6,512]{4,1,3,2,0:T(4,128)(2,1)S(1)}, u32[]{:S(2)}, u32[]{:S(2)}) async-start(bf16[4,4,1,6,512]{4,1,3,2,0:T(4,128)(2,1)} %stack.77), calls=%async_computation.3 | async-start | bytes 196608 | tf_op jit(solution)/shard_map/all_to_all | solution.py:35
  86.1 4.7 %all-to-all-start.17 = ((bf16[2,4,1,6,512]{4,1,3,2,0:T(4,128)(2,1)}), bf16[2,4,1,6,512]{4,1,3,2,0:T(4,128)(2,1)S(1)}, u32[]{:S(2)}, u32[]{:S(2)}) async-start(bf16[2,4,1,6,512]{4,1,3,2,0:T(4,128)(2,1)} %copy.104), calls=%async_computation.17 | async-start | bytes 98304 | tf_op jit(solution)/shard_map/all_to_all | solution.py:35
  98.5 7.6 %all-to-all-start.8 = ((bf16[2,8,1,6,512]{4,1,3,2,0:T(8,128)(2,1)}), bf16[2,8,1,6,512]{4,1,3,2,0:T(8,128)(2,1)S(1)}, u32[]{:S(2)}, u32[]{:S(2)}) async-start(bf16[2,8,1,6,512]{4,1,3,2,0:T(8,128)(2,1)} %pad_maximum_fusion.8), calls=%async_computation.8 | async-start | bytes 196608 | tf_op jit(solution)/shard_map/all_to_all | solution.py:35
  106.1 9.2 %all-to-all-start.13 = ((bf16[2,8,1,7,512]{4,1,3,2,0:T(8,128)(2,1)}), bf16[2,8,1,7,512]{4,1,3,2,0:T(8,128)(2,1)S(1)}, u32[]{:S(2)}, u32[]{:S(2)}) async-start(bf16[2,8,1,7,512]{4,1,3,2,0:T(8,128)(2,1)} %pad_maximum_fusion.6), calls=%async_computation.13 | async-start | bytes 229376 | tf_op jit(solution)/shard_map/all_to_all | solution.py:35
  116.0 9.7 %all-to-all-start.18 = ((bf16[4,8,1,6,512]{4,1,3,2,0:T(8,128)(2,1)}), bf16[4,8,1,6,512]{4,1,3,2,0:T(8,128)(2,1)S(1)}, u32[]{:S(2)}, u32[]{:S(2)}) async-start(bf16[4,8,1,6,512]{4,1,3,2,0:T(8,128)(2,1)} %stack.92), calls=%async_computation.18 | async-start | bytes 393216 | tf_op jit(solution)/shard_map/all_to_all | solution.py:35
  125.7 8.9 %all-to-all-start.14 = ((bf16[2,16,1,7,512]{4,1,3,2,0:T(8,128)(2,1)}), bf16[2,16,1,7,512]{4,1,3,2,0:T(8,128)(2,1)S(1)}, u32[]{:S(2)}, u32[]{:S(2)}) async-start(bf16[2,16,1,7,512]{4,1,3,2,0:T(8,128)(2,1)} %pad_maximum_fusion.4), calls=%async_computation.14 | async-start | bytes 458752 | tf_op jit(solution)/shard_map/all_to_all | solution.py:35
  134.5 15.9 %all-to-all-start = ((bf16[128,2,512]{2,1,0:T(2,128)(2,1)}), bf16[128,2,512]{2,1,0:T(2,128)(2,1)S(1)}, u32[]{:S(2)}, u32[]{:S(2)}) async-start(bf16[128,2,512]{2,1,0:T(2,128)(2,1)} %reshape.156), calls=%async_computation | async-start | bytes 524288 | tf_op jit(solution)/shard_map/all_to_all | solution.py:107
  151.2 10.7 %all-to-all-start.9 = ((bf16[4,16,1,6,512]{4,1,3,2,0:T(8,128)(2,1)}), bf16[4,16,1,6,512]{4,1,3,2,0:T(8,128)(2,1)S(1)}, u32[]{:S(2)}, u32[]{:S(2)}) async-start(bf16[4,16,1,6,512]{4,1,3,2,0:T(8,128)(2,1)} %stack.83), calls=%async_computation.9 | async-start | bytes 786432 | tf_op jit(solution)/shard_map/all_to_all | solution.py:35
  161.9 10.8 %all-to-all-start.19 = ((bf16[2,32,1,6,512]{4,1,3,2,0:T(8,128)(2,1)}), bf16[2,32,1,6,512]{4,1,3,2,0:T(8,128)(2,1)S(1)}, u32[]{:S(2)}, u32[]{:S(2)}) async-start(bf16[2,32,1,6,512]{4,1,3,2,0:T(8,128)(2,1)} %pad_maximum_fusion.3), calls=%async_computation.19 | async-start | bytes 786432 | tf_op jit(solution)/shard_map/all_to_all | solution.py:35
  178.7 12.8 %all-to-all-start.24 = ((bf16[4,16,1,7,512]{4,1,3,2,0:T(8,128)(2,1)}), bf16[4,16,1,7,512]{4,1,3,2,0:T(8,128)(2,1)S(1)}, u32[]{:S(2)}, u32[]{:S(2)}) async-start(bf16[4,16,1,7,512]{4,1,3,2,0:T(8,128)(2,1)} %stack.98), calls=%async_computation.24 | async-start | bytes 917504 | tf_op jit(solution)/shard_map/all_to_all | solution.py:35
  192.5 15.5 %all-to-all-start.5 = ((bf16[4,32,1,6,512]{4,1,3,2,0:T(8,128)(2,1)}), bf16[4,32,1,6,512]{4,1,3,2,0:T(8,128)(2,1)S(1)}, u32[]{:S(2)}, u32[]{:S(2)}) async-start(bf16[4,32,1,6,512]{4,1,3,2,0:T(8,128)(2,1)} %stack.79), calls=%async_computation.5 | async-start | bytes 1572864 | tf_op jit(solution)/shard_map/all_to_all | solution.py:35
  208.0 12.9 %copy-start.2 = (bf16[4,32,1,6,512]{4,1,3,2,0:T(8,128)(2,1)}, bf16[4,32,1,6,512]{4,1,3,2,0:T(8,128)(2,1)S(1)}, u32[]{:S(2)}) copy-start(bf16[4,32,1,6,512]{4,1,3,2,0:T(8,128)(2,1)S(1)} %all-to-all-done.5) | copy-start | bytes 2359300
  208.0 12.9 %all-to-all-start.20 = ((bf16[2,64,1,6,512]{4,1,3,2,0:T(8,128)(2,1)}), bf16[2,64,1,6,512]{4,1,3,2,0:T(8,128)(2,1)S(1)}, u32[]{:S(2)}, u32[]{:S(2)}) async-start(bf16[2,64,1,6,512]{4,1,3,2,0:T(8,128)(2,1)} %pad_maximum_fusion.2), calls=%async_computation.20 | async-start | bytes 1572864 | tf_op jit(solution)/shard_map/all_to_all | solution.py:35
  220.9 0.9 copy-start.3
  221.8 38.0 %all-to-all-start.25 = ((bf16[2,64,1,7,512]{4,1,3,2,0:T(8,128)(2,1)}), bf16[2,64,1,7,512]{4,1,3,2,0:T(8,128)(2,1)S(1)}, u32[]{:S(2)}, u32[]{:S(2)}) async-start(bf16[2,64,1,7,512]{4,1,3,2,0:T(8,128)(2,1)} %pad_maximum_fusion), calls=%async_computation.25 | async-start | bytes 1835008 | tf_op jit(solution)/shard_map/all_to_all | solution.py:35
  225.4 89.7 %collective-permute-start = (bf16[1,1,2048,512]{3,2,1,0:T(8,128)(2,1)}, bf16[1,1,2048,512]{3,2,1,0:T(8,128)(2,1)}, u32[]{:S(2)}, u32[]{:S(2)}) collective-permute-start(bf16[1,1,2048,512]{3,2,1,0:T(8,128)(2,1)} %param.10), channel_id=1, source_target_pairs={{0,8},{8,16},{16,24},{24,32},{32,40},{40,48},{48,56},{56,64},{64,7... | collective-permute-start | bytes 6291464 | tf_op jit(solution)/shard_map/ppermute | solution.py:18
  225.4 89.7 %collective-permute-start.1 = (bf16[1,1,2048,512]{3,2,1,0:T(8,128)(2,1)}, bf16[1,1,2048,512]{3,2,1,0:T(8,128)(2,1)}, u32[]{:S(2)}, u32[]{:S(2)}) collective-permute-start(bf16[1,1,2048,512]{3,2,1,0:T(8,128)(2,1)} %param.10), channel_id=1, source_target_pairs={{8,0},{16,8},{24,16},{32,24},{40,32},{48,40},{56,48},{64,56},{72,6... | collective-permute-start | bytes 6291464 | tf_op jit(solution)/shard_map/ppermute | solution.py:21
  260.8 40.7 %all-to-all-start.15 = ((bf16[4,32,1,7,512]{4,1,3,2,0:T(8,128)(2,1)}), bf16[4,32,1,7,512]{4,1,3,2,0:T(8,128)(2,1)S(1)}, u32[]{:S(2)}, u32[]{:S(2)}) async-start(bf16[4,32,1,7,512]{4,1,3,2,0:T(8,128)(2,1)} %stack.89), calls=%async_computation.15 | async-start | bytes 1835008 | tf_op jit(solution)/shard_map/all_to_all | solution.py:35
  301.6 8.6 %copy-start.1 = (bf16[2,64,1,7,512]{4,1,0,3,2:T(8,128)(2,1)S(1)}, bf16[2,64,1,7,512]{4,1,0,3,2:T(8,128)(2,1)}, u32[]{:S(2)}) copy-start(bf16[2,64,1,7,512]{4,1,0,3,2:T(8,128)(2,1)} %copy.113) | copy-start | bytes 2752516
  314.3 1.6 copy-start.4
